TPU v7x, 32 devices: a whole 2x2x4 slice. The times are simulated.
32 devices in a mesh: groups: 2 (over x), section: 2 (over core), mesh: 8 (over z, y).
Axes of the slice: x: 2, y: 2, z: 4, core: 2. Of those that a mesh axis runs over, the one named last changes fastest.
Arguments:
- inputs: bfloat16 [4, 128, 8192], P('groups', None, 'mesh'), parts along dimension 0, may hold values from -12 to 12
- segments: int32 [4, 128], P('groups'), parts along dimension 0, may hold values from 0 to 3, never falling along the last dimension, each value on 1 to 64 neighbouring positions
- gains: bfloat16 [2, 1, 8192], P('section'), may hold values from 0.25 to 1.75
- w_query: bfloat16 [2, 1, 8192, 1024], P('section', None, None, 'mesh'), may hold values from -1.3258252 to 1.3258252
- w_keyval: bfloat16 [2, 1, 8192, 256], P('section', None, None, 'mesh'), may hold values from -0.055242717 to 0.055242717
- w_output: bfloat16 [2, 1, 1024, 8192], P('section', None, None, 'mesh'), may hold values from -0.1875 to 0.1875
Outputs:
- section_outputs: bfloat16 [2, 4, 128, 8192], P('section', 'groups', None, 'mesh'), parts along dimension 1
There are 2 independent parts, one for each index of `groups`. A program takes and returns all parts, laid end to end along the dimension named above; an argument that names none is the same for every part. Nothing has to cross between parts.
Inputs may be any that keep to these rules, and one draw needn't show every extreme that they name: `segments`: along each micro-batch the document ids never fall; each document spans 1 to 64 positions.
All inputs are finite; a program needn't handle non-finite values.
Results may differ from a plain program's by a relative error of at most 0.0052.
Values may be sent and summed in bfloat16 or wider, within the bound.
A program may use at most 64 MiB of HBM per device.

v0:
```python
import jax
import jax.numpy as jnp
from jax import lax
from jax.sharding import PartitionSpec as P

HD = 128
GROUP = 8


norm_epsilon = 1e-05
rope_theta = 500000.0


def partner_2(x, axis, distance):
    return lax.ppermute(x, axis, [(i, i ^ 1 << distance) for i in range(lax.axis_size(axis))])


def from_behind(block, axis, distance):
    devices = range(lax.axis_size(axis))
    route = [(i - distance, i) for i in devices if i - distance in devices]
    return lax.ppermute(block, axis, route)


def position_tables(segment_row):
    row_length = segment_row.shape[0]
    indices = jnp.arange(row_length, dtype=jnp.int32)
    doc_starts = jnp.concatenate([jnp.ones((1,), dtype=bool), segment_row[1:] != segment_row[:-1]])
    first_index = lax.cummax(jnp.where(doc_starts, indices, jnp.zeros_like(indices)), axis=0)
    positions = (indices - first_index).astype(jnp.float32)
    half_width = HD // 2
    freqs = rope_theta ** (-(2.0 * jnp.arange(half_width, dtype=jnp.float32)) / HD)
    angles = positions[:, None] * freqs[None, :]
    cosine_table = jnp.concatenate([jnp.cos(angles), jnp.cos(angles)], axis=1)
    sine_table = jnp.concatenate([jnp.sin(angles), jnp.sin(angles)], axis=1)
    allowed = (indices[None, :] <= indices[:, None]) & (
        segment_row[None, :] == segment_row[:, None]
    )
    return (cosine_table, sine_table, allowed)


def rotate(values, cosine_table, sine_table):
    half_width = values.shape[-1] // 2
    turned = jnp.concatenate([-values[..., half_width:], values[..., :half_width]], axis=-1)
    return values * cosine_table + turned * sine_table


def softmax_weights(scores, allowed):
    masked = jnp.where(allowed, scores, -1e30)
    highest = jnp.max(masked, axis=-1, keepdims=True)
    raised = jnp.exp(masked - highest)
    return (raised / jnp.sum(raised, axis=-1, keepdims=True)).astype(jnp.bfloat16)


def apply_layer(
    activations,
    gain_row,
    query_weight,
    keyval_weight,
    output_weight,
    cosine_table,
    sine_table,
    allowed,
    mesh_index,
):
    floats = activations.astype(jnp.float32)
    gathered = lax.all_gather(activations, "mesh", axis=1, tiled=True)
    whole_floats = gathered.astype(jnp.float32)
    scale = lax.rsqrt(jnp.mean(whole_floats * whole_floats, axis=1, keepdims=True) + norm_epsilon)
    normed = (whole_floats * scale * gain_row.astype(jnp.float32)).astype(jnp.bfloat16)
    query_raw = jnp.dot(normed, query_weight, preferred_element_type=jnp.float32)
    keyval_raw = jnp.dot(normed, keyval_weight, preferred_element_type=jnp.float32)
    query = rotate(query_raw, cosine_table, sine_table).astype(jnp.bfloat16)
    keyval_part = keyval_raw.astype(jnp.bfloat16)
    for bit_index in range(GROUP.bit_length() - 1):
        partner = partner_2(keyval_part, "mesh", bit_index)
        upper_half = mesh_index // (1 << bit_index) % 2 == 1
        keyval_part = jnp.where(
            upper_half,
            jnp.concatenate([partner, keyval_part], axis=1),
            jnp.concatenate([keyval_part, partner], axis=1),
        )
    keys = rotate(keyval_part[:, :HD].astype(jnp.float32), cosine_table, sine_table).astype(
        jnp.bfloat16
    )
    values = keyval_part[:, HD:]
    scores = jnp.dot(query, keys.T, preferred_element_type=jnp.float32) * HD ** (-0.5)
    probs = softmax_weights(scores, allowed)
    attended = jnp.dot(probs, values, preferred_element_type=jnp.float32).astype(jnp.bfloat16)
    mixed = jnp.dot(
        lax.all_gather(attended, "mesh", axis=1, tiled=True),
        output_weight,
        preferred_element_type=jnp.float32,
    )
    return (floats + mixed).astype(jnp.bfloat16)


def shards(inputs, segments, gains, w_query, w_keyval, w_output):
    micro_count, row_count, local_cols = inputs.shape
    section_count = lax.axis_size("section")
    section_index = lax.axis_index("section")
    mesh_index = lax.axis_index("mesh")
    cosine_list, sine_list, allowed_list = ([], [], [])
    for micro_index in range(micro_count):
        cosine_table, sine_table, allowed = position_tables(segments[micro_index])
        cosine_list.append(cosine_table)
        sine_list.append(sine_table)
        allowed_list.append(allowed)
    cosine_all = jnp.stack(cosine_list)
    sine_all = jnp.stack(sine_list)
    allowed_all = jnp.stack(allowed_list)
    step_count = micro_count + section_count - 1
    received = jnp.zeros((row_count, local_cols), jnp.bfloat16)
    results = []
    for section_step in range(step_count):
        feed_slot = min(section_step, micro_count - 1)
        micro_here = jnp.clip(section_step - section_index, 0, micro_count - 1)
        cosine_table = lax.dynamic_index_in_dim(cosine_all, micro_here, 0, keepdims=False)
        sine_table = lax.dynamic_index_in_dim(sine_all, micro_here, 0, keepdims=False)
        allowed = lax.dynamic_index_in_dim(allowed_all, micro_here, 0, keepdims=False)
        current = jnp.where(section_index == 0, inputs[feed_slot], received)
        current = apply_layer(
            current,
            gains[0, 0],
            w_query[0, 0],
            w_keyval[0, 0],
            w_output[0, 0],
            cosine_table,
            sine_table,
            allowed,
            mesh_index,
        )
        results.append(current)
        if section_step + 1 < step_count:
            received = from_behind(current, "section", 1)
    stacked = jnp.stack(results)
    chosen = lax.dynamic_slice_in_dim(stacked, section_index, micro_count, 0)
    return chosen[None]


def solution(mesh):
    return jax.shard_map(
        shards,
        mesh=mesh,
        in_specs=(
            P("groups", None, "mesh"),
            P("groups", None),
            P("section", None, None),
            P("section", None, None, "mesh"),
            P("section", None, None, "mesh"),
            P("section", None, None, "mesh"),
        ),
        out_specs=P("section", "groups", None, "mesh"),
        check_vma=False,
    )
```

profile of v0, /device:TPU:0, one launch (start us, length us, event | category | flops | bytes accessed | tf_op | source)
XLA Modules:
  0.0 303.9 jit_solution(13265245721027685720)
XLA Ops:
  6.5 1.8 slice_select_fusion
  8.4 0.8 convert_element_type.150
  9.2 0.9 compare_bitcast_fusion
  11.1 0.3 multiply_sine_fusion
  11.4 0.8 slice_bitcast_fusion
  12.3 49.1 %all-gather.9.cloned.1.call-done = bf16[1,128,8192]{2,1,0:T(8,128)(2,1)} async-done(((bf16[1,128,1024]{2,1,0:T(8,128)(2,1)}), bf16[1,128,8192]{2,1,0:T(8,128)(2,1)}) %all-gather.9.cloned.1.call-update) | async-done | bytes 2097168 | tf_op jit(solution)/shard_map/all_gather | solution.py:66
  61.3 2.2 fusion.6
  63.6 0.9 convolution_convert_fusion.5
  64.5 0.6 collective-permute-start
  65.1 3.1 %collective-permute-done = bf16[128,32]{0,1:T(8,128)(2,1)S(1)} collective-permute-done((bf16[128,32]{0,1:T(8,128)(2,1)S(1)}, bf16[128,32]{0,1:T(8,128)(2,1)S(1)}, u32[]{:S(2)}, u32[]{:S(2)}) %collective-permute-start) | collective-permute-done | bytes 8224 | tf_op jit(solution)/shard_map/ppermute | solution.py:15
  68.2 1.6 collective-permute-start.1
  69.8 3.3 %fusion.19 = f32[128,128]{0,1:T(8,128)S(1)} fusion(bf16[1,1,8192,128]{3,2,1,0:T(8,128)(2,1)} %param.9, bf16[1,128,8192]{2,1,0:T(8,128)(2,1)} %all-gather.9.cloned.1.call-done, f32[8192]{0:T(1024)S(1)} %bitcast.148, f32[128]{0:T(128)S(1)} %add_rsqrt_fusion.2), kind=kOutput, calls=%fused_computation.25 | convolution fusion | flops 272629760 | bytes 4293120 | tf_op jit(solution)/shard_map/dot_general | solution.py:70
  73.2 1.0 collective-permute-start.2
  74.1 4.2 %collective-permute-done.2 = bf16[128,128]{0,1:T(8,128)(2,1)S(1)} collective-permute-done((bf16[128,128]{0,1:T(8,128)(2,1)S(1)}, bf16[128,128]{0,1:T(8,128)(2,1)S(1)}, u32[]{:S(2)}, u32[]{:S(2)}) %collective-permute-start.2) | collective-permute-done | bytes 32800 | tf_op jit(solution)/shard_map/ppermute | solution.py:15
  78.4 0.3 fusion.107
  78.9 26.5 %all_gather.19 = bf16[128,1024]{1,0:T(8,128)(2,1)S(1)} all-gather(bf16[128,128]{1,0:T(8,128)(2,1)S(1)} %convolution_convert_fusion.2), channel_id=1, replica_groups=mesh['groups'=2,'section'=2,'mesh'=8] {'mesh'}, dimensions={1}, use_global_device_ids=true | all-gather | bytes 294912 | tf_op jit(solution)/shard_map/all_gather | solution.py:90
  105.4 0.4 fusion.24
  105.9 1.3 collective-permute-start.3
  107.2 1.1 collective-permute-done.3
  108.3 0.7 bitcast_select_fusion.1
  109.1 46.4 %all-gather.5.cloned.1.call-done = bf16[128,8192]{1,0:T(8,128)(2,1)} async-done(((bf16[128,1024]{1,0:T(8,128)(2,1)}), bf16[128,8192]{1,0:T(8,128)(2,1)}) %all-gather.5.cloned.1.call-update) | async-done | bytes 2097168 | tf_op jit(solution)/shard_map/all_gather | solution.py:66
  155.6 2.2 fusion
  157.8 2.0 convolution_convert_fusion.4
  159.8 0.6 collective-permute-start.4
  160.4 3.1 %collective-permute-done.4 = bf16[128,32]{0,1:T(8,128)(2,1)S(1)} collective-permute-done((bf16[128,32]{0,1:T(8,128)(2,1)S(1)}, bf16[128,32]{0,1:T(8,128)(2,1)S(1)}, u32[]{:S(2)}, u32[]{:S(2)}) %collective-permute-start.4) | collective-permute-done | bytes 8224 | tf_op jit(solution)/shard_map/ppermute | solution.py:15
  163.5 1.6 collective-permute-start.5
  165.1 3.3 %fusion.17 = f32[128,128]{0,1:T(8,128)S(1)} fusion(bf16[1,1,8192,128]{3,2,1,0:T(8,128)(2,1)} %param.9, bf16[128,8192]{1,0:T(8,128)(2,1)} %all-gather.5.cloned.1.call-done, f32[128]{0:T(128)S(1)} %add_rsqrt_fusion.1, f32[8192]{0:T(1024)S(1)} %bitcast.150), kind=kOutput, calls=%fused_computation.23 | convolution fusion | flops 272629760 | bytes 4293120 | tf_op jit(solution)/shard_map/dot_general | solution.py:70
  168.4 1.0 collective-permute-start.6
  169.4 4.2 %collective-permute-done.6 = bf16[128,128]{0,1:T(8,128)(2,1)S(1)} collective-permute-done((bf16[128,128]{0,1:T(8,128)(2,1)S(1)}, bf16[128,128]{0,1:T(8,128)(2,1)S(1)}, u32[]{:S(2)}, u32[]{:S(2)}) %collective-permute-start.6) | collective-permute-done | bytes 32800 | tf_op jit(solution)/shard_map/ppermute | solution.py:15
  173.6 0.3 fusion.108
  174.1 26.5 %all_gather.21 = bf16[128,1024]{1,0:T(8,128)(2,1)S(1)} all-gather(bf16[128,128]{1,0:T(8,128)(2,1)S(1)} %convolution_convert_fusion.1), channel_id=1, replica_groups=mesh['groups'=2,'section'=2,'mesh'=8] {'mesh'}, dimensions={1}, use_global_device_ids=true | all-gather | bytes 294912 | tf_op jit(solution)/shard_map/all_gather | solution.py:90
  200.6 0.4 add_convert_fusion.1
  201.1 1.3 collective-permute-start.7
  202.4 1.1 collective-permute-done.7
  203.5 0.7 bitcast_select_fusion
  204.3 46.5 %all-gather.7.cloned.1.call-done = bf16[128,8192]{1,0:T(8,128)(2,1)} async-done(((bf16[128,1024]{1,0:T(8,128)(2,1)}), bf16[128,8192]{1,0:T(8,128)(2,1)}) %all-gather.7.cloned.1.call-update) | async-done | bytes 2097168 | tf_op jit(solution)/shard_map/all_gather | solution.py:66
  250.8 2.2 fusion.3
  253.0 2.0 convolution_convert_fusion.3
  255.0 0.6 collective-permute-start.8
  255.6 3.1 %collective-permute-done.8 = bf16[128,32]{0,1:T(8,128)(2,1)S(1)} collective-permute-done((bf16[128,32]{0,1:T(8,128)(2,1)S(1)}, bf16[128,32]{0,1:T(8,128)(2,1)S(1)}, u32[]{:S(2)}, u32[]{:S(2)}) %collective-permute-start.8) | collective-permute-done | bytes 8224 | tf_op jit(solution)/shard_map/ppermute | solution.py:15
  258.7 1.6 collective-permute-start.9
  260.3 3.3 %fusion.15 = f32[128,128]{0,1:T(8,128)S(1)} fusion(bf16[1,1,8192,128]{3,2,1,0:T(8,128)(2,1)} %param.9, bf16[128,8192]{1,0:T(8,128)(2,1)} %all-gather.7.cloned.1.call-done, f32[128]{0:T(128)S(1)} %add_rsqrt_fusion, f32[8192]{0:T(1024)S(1)} %bitcast.152), kind=kOutput, calls=%fused_computation.21 | convolution fusion | flops 272629760 | bytes 4293120 | tf_op jit(solution)/shard_map/dot_general | solution.py:70
  263.6 1.0 collective-permute-start.10
  264.6 4.2 %collective-permute-done.10 = bf16[128,128]{0,1:T(8,128)(2,1)S(1)} collective-permute-done((bf16[128,128]{0,1:T(8,128)(2,1)S(1)}, bf16[128,128]{0,1:T(8,128)(2,1)S(1)}, u32[]{:S(2)}, u32[]{:S(2)}) %collective-permute-start.10) | collective-permute-done | bytes 32800 | tf_op jit(solution)/shard_map/ppermute | solution.py:15
  268.9 0.2 fusion.109
  269.3 26.5 %all_gather.23 = bf16[128,1024]{1,0:T(8,128)(2,1)S(1)} all-gather(bf16[128,128]{1,0:T(8,128)(2,1)S(1)} %convolution_convert_fusion), channel_id=1, replica_groups=mesh['groups'=2,'section'=2,'mesh'=8] {'mesh'}, dimensions={1}, use_global_device_ids=true | all-gather | bytes 294912 | tf_op jit(solution)/shard_map/all_gather | solution.py:90
  295.9 0.4 fusion.42
  296.3 1.1 fusion.38
  (69 shorter events, 2.1 us)
Async XLA Ops:
  6.5 98.9 %copy-start = (bf16[1,1,1024,1024]{3,2,1,0:T(8,128)(2,1)S(1)}, bf16[1,1,1024,1024]{3,2,1,0:T(8,128)(2,1)}, u32[]{:S(2)}) copy-start(bf16[1,1,1024,1024]{3,2,1,0:T(8,128)(2,1)} %param.11) | copy-start | bytes 6291460
  6.5 57.0 %copy-start.8 = (bf16[1,1,8192,32]{2,3,1,0:T(8,128)(2,1)S(1)}, bf16[1,1,8192,32]{2,3,1,0:T(8,128)(2,1)}, u32[]{:S(2)}) copy-start(bf16[1,1,8192,32]{2,3,1,0:T(8,128)(2,1)} %param.10) | copy-start | bytes 1572868
  6.5 54.8 %all-gather.9.cloned.1.call-start = ((), (), s32[]{:S(2)}) async-start(), calls=%async_computation.2 | async-start | bytes 2359296 | tf_op jit(solution)/shard_map/all_gather | solution.py:66
  8.4 147.2 %all-gather.5.cloned.1.call-start = ((), (), s32[]{:S(2)}) async-start(), calls=%async_computation | async-start | bytes 2359296 | tf_op jit(solution)/shard_map/all_gather | solution.py:66
  61.3 2.3 copy-start.4
  64.5 3.7 %collective-permute-start = (bf16[128,32]{0,1:T(8,128)(2,1)S(1)}, bf16[128,32]{0,1:T(8,128)(2,1)S(1)}, u32[]{:S(2)}, u32[]{:S(2)}) collective-permute-start(bf16[128,32]{0,1:T(8,128)(2,1)S(1)} %convolution_convert_fusion.5), channel_id=1, source_target_pairs={{0,1},{1,0},{2,3},{3,2},{4,5},{5,4},{6,7},{7,6},{8,9},{9,8},{10,11... | collective-permute-start | bytes 24584 | tf_op jit(solution)/shard_map/ppermute | solution.py:15
  68.2 4.9 %collective-permute-start.1 = (bf16[128,64]{0,1:T(8,128)(2,1)S(1)}, bf16[128,64]{0,1:T(8,128)(2,1)S(1)}, u32[]{:S(2)}, u32[]{:S(2)}) collective-permute-start(bf16[128,64]{0,1:T(8,128)(2,1)S(1)} %maximum_select_fusion.6), channel_id=1, source_target_pairs={{0,2},{1,3},{2,0},{3,1},{4,6},{5,7},{6,4},{7,5},{8,10},{9,11},{10,... | collective-permute-start | bytes 49160 | tf_op jit(solution)/shard_map/ppermute | solution.py:15
  73.1 32.3 %copy-start.1 = (bf16[1,128,1024]{2,1,0:T(8,128)(2,1)S(1)}, bf16[1,128,1024]{2,1,0:T(8,128)(2,1)}, u32[]{:S(2)}) copy-start(bf16[1,128,1024]{2,1,0:T(8,128)(2,1)} %slice_select_fusion) | copy-start | bytes 786436
  73.2 5.2 %collective-permute-start.2 = (bf16[128,128]{0,1:T(8,128)(2,1)S(1)}, bf16[128,128]{0,1:T(8,128)(2,1)S(1)}, u32[]{:S(2)}, u32[]{:S(2)}) collective-permute-start(bf16[128,128]{0,1:T(8,128)(2,1)S(1)} %maximum_select_fusion.3), channel_id=1, source_target_pairs={{0,4},{1,5},{2,6},{3,7},{4,0},{5,1},{6,2},{7,3},{8,12},{9,13},{10,... | collective-permute-start | bytes 98312 | tf_op jit(solution)/shard_map/ppermute | solution.py:15
  78.4 29.9 %copy-start.7 = (bf16[2,128,1024]{2,1,0:T(8,128)(2,1)S(1)}, bf16[2,128,1024]{2,1,0:T(8,128)(2,1)}, u32[]{:S(2)}) copy-start(bf16[2,128,1024]{2,1,0:T(8,128)(2,1)} %param.6) | copy-start | bytes 1572868
  105.9 2.4 collective-permute-start.3
  109.1 141.7 %all-gather.7.cloned.1.call-start = ((), (), s32[]{:S(2)}) async-start(), calls=%async_computation.1 | async-start | bytes 2359296 | tf_op jit(solution)/shard_map/all_gather | solution.py:66
  155.6 2.2 copy-start.6
  159.8 3.7 %collective-permute-start.4 = (bf16[128,32]{0,1:T(8,128)(2,1)S(1)}, bf16[128,32]{0,1:T(8,128)(2,1)S(1)}, u32[]{:S(2)}, u32[]{:S(2)}) collective-permute-start(bf16[128,32]{0,1:T(8,128)(2,1)S(1)} %convolution_convert_fusion.4), channel_id=1, source_target_pairs={{0,1},{1,0},{2,3},{3,2},{4,5},{5,4},{6,7},{7,6},{8,9},{9,8},{10,11... | collective-permute-start | bytes 24584 | tf_op jit(solution)/shard_map/ppermute | solution.py:15
  163.5 4.9 %collective-permute-start.5 = (bf16[128,64]{0,1:T(8,128)(2,1)S(1)}, bf16[128,64]{0,1:T(8,128)(2,1)S(1)}, u32[]{:S(2)}, u32[]{:S(2)}) collective-permute-start(bf16[128,64]{0,1:T(8,128)(2,1)S(1)} %maximum_select_fusion.7), channel_id=1, source_target_pairs={{0,2},{1,3},{2,0},{3,1},{4,6},{5,7},{6,4},{7,5},{8,10},{9,11},{10,... | collective-permute-start | bytes 49160 | tf_op jit(solution)/shard_map/ppermute | solution.py:15
  168.4 32.3 %copy-start.3 = (bf16[128,1024]{1,0:T(8,128)(2,1)S(1)}, bf16[128,1024]{1,0:T(8,128)(2,1)}, u32[]{:S(2)}) copy-start(bf16[128,1024]{1,0:T(8,128)(2,1)} %bitcast_select_fusion.1) | copy-start | bytes 786436
  168.4 5.2 %collective-permute-start.6 = (bf16[128,128]{0,1:T(8,128)(2,1)S(1)}, bf16[128,128]{0,1:T(8,128)(2,1)S(1)}, u32[]{:S(2)}, u32[]{:S(2)}) collective-permute-start(bf16[128,128]{0,1:T(8,128)(2,1)S(1)} %maximum_select_fusion.4), channel_id=1, source_target_pairs={{0,4},{1,5},{2,6},{3,7},{4,0},{5,1},{6,2},{7,3},{8,12},{9,13},{10,... | collective-permute-start | bytes 98312 | tf_op jit(solution)/shard_map/ppermute | solution.py:15
  201.1 2.4 collective-permute-start.7
  250.8 2.2 copy-start.5
  255.0 3.7 %collective-permute-start.8 = (bf16[128,32]{0,1:T(8,128)(2,1)S(1)}, bf16[128,32]{0,1:T(8,128)(2,1)S(1)}, u32[]{:S(2)}, u32[]{:S(2)}) collective-permute-start(bf16[128,32]{0,1:T(8,128)(2,1)S(1)} %convolution_convert_fusion.3), channel_id=1, source_target_pairs={{0,1},{1,0},{2,3},{3,2},{4,5},{5,4},{6,7},{7,6},{8,9},{9,8},{10,11... | collective-permute-start | bytes 24584 | tf_op jit(solution)/shard_map/ppermute | solution.py:15
  258.7 4.9 %collective-permute-start.9 = (bf16[128,64]{0,1:T(8,128)(2,1)S(1)}, bf16[128,64]{0,1:T(8,128)(2,1)S(1)}, u32[]{:S(2)}, u32[]{:S(2)}) collective-permute-start(bf16[128,64]{0,1:T(8,128)(2,1)S(1)} %maximum_select_fusion.8), channel_id=1, source_target_pairs={{0,2},{1,3},{2,0},{3,1},{4,6},{5,7},{6,4},{7,5},{8,10},{9,11},{10,... | collective-permute-start | bytes 49160 | tf_op jit(solution)/shard_map/ppermute | solution.py:15
  263.6 32.3 %copy-start.2 = (bf16[128,1024]{1,0:T(8,128)(2,1)S(1)}, bf16[128,1024]{1,0:T(8,128)(2,1)}, u32[]{:S(2)}) copy-start(bf16[128,1024]{1,0:T(8,128)(2,1)} %bitcast_select_fusion) | copy-start | bytes 786436
  263.6 5.2 %collective-permute-start.10 = (bf16[128,128]{0,1:T(8,128)(2,1)S(1)}, bf16[128,128]{0,1:T(8,128)(2,1)S(1)}, u32[]{:S(2)}, u32[]{:S(2)}) collective-permute-start(bf16[128,128]{0,1:T(8,128)(2,1)S(1)} %maximum_select_fusion.5), channel_id=1, source_target_pairs={{0,4},{1,5},{2,6},{3,7},{4,0},{5,1},{6,2},{7,3},{8,12},{9,13},{10,... | collective-permute-start | bytes 98312 | tf_op jit(solution)/shard_map/ppermute | solution.py:15
Sparse Core Ops, SparseCore 0:
  9.5 51.7 all-gather.8
  109.2 46.3 all-gather.4
  204.4 46.3 all-gather.6
where the time goes:
time: 304 us
  waiting for transfers between devices  166 us (55%)
  blocking collectives  79.6 us (26%)
  matrix products  17.5 us (6%)
  other arithmetic  14.2 us (5%)
  between operations  13.5 us (4%)
  starting transfers between devices  12.1 us (4%)
    all_gather x3, waiting for transfers between devices, apply_layer(): gathered = lax.all_gather(activations, 'mesh', axis=1, tiled=True)  142 us
    all_gather x3, blocking collectives, apply_layer(): lax.all_gather(attended, 'mesh', axis=1, tiled=True)  79.6 us
    ppermute x9, waiting for transfers between devices, partner_2(): lax.ppermute(x, axis, [(i, i ^ 1 << distance) for i in range(lax.axis_siz...  21.9 us
    dot_general x3, matrix products, apply_layer(): jnp.dot(normed, query_weight, preferred_element_type=jnp.float32)  9.91 us
    ppermute x9, starting transfers between devices, partner_2(): lax.ppermute(x, axis, [(i, i ^ 1 << distance) for i in range(lax.axis_siz...  9.36 us
    reduce_sum x3, other arithmetic, apply_layer(): jnp.mean(whole_floats * whole_floats, axis=1, keepdims=True) + norm_epsilon  6.68 us
  transfers between devices with their start and end apart: 14, of which 11 were waited for; matrix products, arithmetic and copies ran while one was open for 5% of the time, Pallas kernels for 0%

commit v1 on v0

v1 whole, which is shorter than its diff:
```python
import functools
import math

import jax
import jax.numpy as jnp
import numpy as np
from jax import lax
from jax.experimental import pallas as pl
from jax.experimental.pallas import tpu as pltpu
from jax.sharding import PartitionSpec as P

HD = 128
GROUP = 8
norm_epsilon = 1e-05
rope_theta = 500000.0
MESH = pl.DeviceIdType.MESH
F32 = jnp.float32
BF16 = jnp.bfloat16


def inner_of(n):
    inner = 1
    while inner * 2 * inner * 2 <= n:
        inner *= 2
    return inner


def kernel(
    n,
    x_hbm,
    seg_ref,
    freq_ref,
    g_hbm,
    wq_hbm,
    wkv_hbm,
    wo_hbm,
    out_ref,
    xbuf,
    wq,
    wkv,
    wo,
    gbuf,
    ssq,
    kvbuf,
    att,
    fin,
    acc,
    scale_ref,
    cos_ref,
    sin_ref,
    mask_ref,
    in_sem,
    w_sem,
    w_send,
    x_recv,
    z_send,
    y_send,
    ssq_recv,
    ssq_send,
    kv_recv,
    kv_send,
    att_recv,
    att_send,
    out_send,
    out_recv,
    out_local,
):
    core = lax.axis_index("section")
    me = lax.axis_index("mesh")
    other = 1 - core
    inner = inner_of(n)
    outer = n // inner
    row, lane = me // inner, me % inner
    tok, cols = x_hbm.shape[1:]
    width = n * cols
    kvw = wkv_hbm.shape[1]
    first = me // GROUP * GROUP

    def block(layer, src):
        return xbuf.at[layer, :, pl.ds(pl.multiple_of(src * cols, cols), cols)]

    def send_to(src, dst, send, recv, peer):
        return pltpu.make_async_remote_copy(
            src_ref=src, dst_ref=dst, send_sem=send, recv_sem=recv,
            device_id={"mesh": peer}, device_id_type=MESH,
        )

    load_x = pltpu.make_async_copy(x_hbm.at[core], block(0, me), in_sem)
    load_x.start()
    weights = ((g_hbm, gbuf), (wq_hbm, wq), (wkv_hbm, wkv), (wo_hbm, wo))
    own_weights = [
        pltpu.make_async_copy(src, dst.at[core], w_sem.at[core, k]) for k, (src, dst) in enumerate(weights)
    ]
    sent_weights = [
        pltpu.make_async_remote_copy(
            src_ref=src, dst_ref=dst.at[core], send_sem=w_send.at[k], recv_sem=w_sem.at[core, k],
            device_id={"section": other}, device_id_type=MESH,
        )
        for k, (src, dst) in enumerate(weights)
    ]
    for copy in own_weights:
        copy.start()

    barrier = pltpu.get_barrier_semaphore()

    def greet(k, carry):
        pl.semaphore_signal(barrier, inc=1, device_id={"mesh": (me + k) % n}, device_id_type=MESH)
        return carry

    lax.fori_loop(1, n, greet, 0)
    pl.semaphore_signal(barrier, inc=1, device_id={"section": other}, device_id_type=MESH)
    load_x.wait()
    pl.semaphore_wait(barrier, n)

    def z_copy(layer, src, sign):
        return send_to(
            block(layer, src), block(layer, src), z_send.at[layer, (sign + 1) // 2, src // inner],
            x_recv.at[layer, src], me + sign * inner,
        )

    def y_copy(layer, src, k):
        return send_to(
            block(layer, src), block(layer, src), y_send.at[layer, k, src // inner],
            x_recv.at[layer, src], row * inner + (lane + k) % inner,
        )

    def arrived(layer, src):
        y_copy(layer, src, 0).wait_recv()

    def over_y(body):
        if inner == 2:
            body(1)
        else:
            def step(k, carry):
                body(k)
                return carry
            lax.fori_loop(1, inner, step, 0)

    def forward(layer, src, signs):
        for sign in signs:
            @pl.when((row + sign >= 0) & (row + sign < outer))
            def _():
                z_copy(layer, src, sign).start()
        over_y(lambda k: y_copy(layer, src, k).start())

    def over_peers(total, base, mine, body):
        def step(k, carry):
            body(base + (mine - base + k) % total)
            return carry
        lax.fori_loop(1, total, step, 0)

    def ssq_copy(layer, peer):
        return send_to(ssq.at[layer, me], ssq.at[layer, me], ssq_send.at[layer, peer], ssq_recv.at[layer, me], peer)

    def ssq_wait(layer, peer):
        send_to(ssq.at[layer, peer], ssq.at[layer, peer], ssq_send.at[layer, peer], ssq_recv.at[layer, peer], peer).wait_recv()

    def send_own(layer, value):
        floats = value.astype(F32)
        total = jnp.sum(floats * floats, axis=1, keepdims=True)
        ssq[layer, me] = jnp.transpose(jnp.broadcast_to(total, (tok, tok)))[:8]
        over_peers(n, 0, me, lambda peer: ssq_copy(layer, peer).start())
        forward(layer, me, (1, -1))

    send_own(0, block(0, me)[...])
    for copy in sent_weights:
        copy.start()

    seg = jnp.broadcast_to(seg_ref[pl.ds(core, 1), :].astype(F32), (tok, tok))
    t_index = lax.broadcasted_iota(jnp.int32, (tok, tok), 0)
    u_index = lax.broadcasted_iota(jnp.int32, (tok, tok), 1)
    allowed = jnp.where((seg == jnp.transpose(seg)) & (u_index <= t_index), 1.0, 0.0)
    mask_ref[...] = allowed
    positions = jnp.sum(allowed, axis=1, keepdims=True) - 1.0
    angles = positions * freq_ref[0:1, :]
    cos_ref[...] = jnp.cos(angles)
    sine = jnp.sin(angles)
    head_lane = lax.broadcasted_iota(jnp.int32, (tok, HD), 1)
    sin_ref[...] = jnp.where(head_lane < HD // 2, -sine, sine)

    def rope(values):
        return (values * cos_ref[...] + pltpu.roll(values, HD // 2, 1) * sin_ref[...]).astype(BF16)

    def weight_wait(layer, k):
        src, dst = weights[k]
        pltpu.make_async_copy(src, dst.at[layer], w_sem.at[layer, k]).wait()

    def consume(layer, src):
        span = pl.ds(pl.multiple_of(src * cols, cols), cols)
        scale = jnp.concatenate([scale_ref[...]] * (cols // HD), axis=1)
        normed = (xbuf[layer, :, span].astype(F32) * scale * gbuf[layer, :, span].astype(F32)).astype(BF16)
        both = jnp.concatenate([wq[layer, span, :], wkv[layer, span, :]], axis=1)
        acc[...] += jnp.dot(normed, both, preferred_element_type=F32)

    for layer in range(2):
        over_peers(n, 0, me, lambda peer: ssq_wait(layer, peer))
        total = jnp.sum(ssq[layer], axis=0)
        scale_ref[...] = jnp.transpose(
            jnp.broadcast_to(lax.rsqrt(total[0:1, :] * (1.0 / width) + norm_epsilon), (HD, tok))
        )
        for k in range(3):
            weight_wait(layer, k)
        acc[...] = jnp.zeros_like(acc)
        consume(layer, me)

        def side_blocks(distance):
            for sign in (1, -1):
                src_row = row - sign * distance

                @pl.when((src_row >= 0) & (src_row < outer))
                def _():
                    def take(k):
                        src = src_row * inner + (lane + k) % inner
                        arrived(layer, src)
                        consume(layer, src)
                    over_y(take)

        def wave(distance, carry):
            for sign in (1, -1):
                src_row = row - sign * distance

                @pl.when((src_row >= 0) & (src_row < outer))
                def _():
                    src = src_row * inner + lane
                    arrived(layer, src)
                    forward(layer, src, (sign,))
                    consume(layer, src)

            @pl.when(distance > 1)
            def _():
                side_blocks(distance - 1)
            return carry

        def take_own_row(k):
            src = row * inner + (lane + k) % inner
            arrived(layer, src)
            consume(layer, src)

        lax.fori_loop(1, 2, wave, 0)
        over_y(take_own_row)
        lax.fori_loop(2, outer, wave, 0)
        side_blocks(outer - 1)

        kvbuf[layer, me - first] = acc[:, HD:].astype(BF16)

        def kv_copy(peer):
            return send_to(
                kvbuf.at[layer, me - first], kvbuf.at[layer, me - first],
                kv_send.at[layer, peer - first], kv_recv.at[layer, me - first], peer,
            )

        def kv_wait(peer):
            send_to(
                kvbuf.at[layer, peer - first], kvbuf.at[layer, peer - first],
                kv_send.at[layer, peer - first], kv_recv.at[layer, peer - first], peer,
            ).wait_recv()

        over_peers(GROUP, first, me, lambda peer: kv_copy(peer).start())
        query = rope(acc[:, :HD])
        over_peers(GROUP, first, me, kv_wait)
        keyval = jnp.concatenate([kvbuf[layer, j] for j in range(GROUP)], axis=1)
        keys = rope(keyval[:, :HD].astype(F32))
        scores = lax.dot_general(
            query, keys, (((1,), (1,)), ((), ())), preferred_element_type=F32
        ) * HD ** (-0.5)
        masked = jnp.where(mask_ref[...] > 0.0, scores, -1e30)
        raised = jnp.exp(masked - jnp.max(masked, axis=1, keepdims=True))
        probs = (raised / jnp.sum(raised, axis=1, keepdims=True)).astype(BF16)
        attended = jnp.dot(probs, keyval[:, HD:], preferred_element_type=F32).astype(BF16)

        def att_block(src):
            return att.at[layer, :, pl.ds(pl.multiple_of(src * HD, HD), HD)]

        def att_copy(peer):
            return send_to(att_block(me), att_block(me), att_send.at[layer, peer], att_recv.at[layer, me], peer)

        def att_wait(peer):
            send_to(att_block(peer), att_block(peer), att_send.at[layer, peer], att_recv.at[layer, peer], peer).wait_recv()

        att_block(me)[...] = attended
        over_peers(n, 0, me, lambda peer: att_copy(peer).start())
        weight_wait(layer, 3)
        over_peers(n, 0, me, att_wait)
        mixed = jnp.dot(att[layer], wo[layer], preferred_element_type=F32)
        result = (block(layer, me)[...].astype(F32) + mixed).astype(BF16)
        if layer == 0:
            block(1, me)[...] = result
            send_own(1, result)
            kept = block(1, me)
        else:
            fin[...] = result
            kept = fin

        @pl.when(core == layer)
        def _():
            pltpu.make_async_copy(kept, out_ref.at[core], out_local).start()

        @pl.when(core != layer)
        def _():
            pltpu.make_async_remote_copy(
                src_ref=kept, dst_ref=out_ref.at[core], send_sem=out_send, recv_sem=out_recv,
                device_id={"section": other}, device_id_type=MESH,
            ).start()

        over_peers(GROUP, first, me, lambda peer: kv_copy(peer).wait_send())
        over_peers(n, 0, me, lambda peer: att_copy(peer).wait_send())

    for layer in range(2):
        over_peers(n, 0, me, lambda peer: ssq_copy(layer, peer).wait_send())

        def drain(src_row, carry):
            src = src_row * inner + lane

            @pl.when((src_row <= row) & (row + 1 < outer))
            def _():
                z_copy(layer, src, 1).wait_send()

            @pl.when((src_row >= row) & (row >= 1))
            def _():
                z_copy(layer, src, -1).wait_send()

            over_y(lambda k: y_copy(layer, src, k).wait_send())
            return carry

        lax.fori_loop(0, outer, drain, 0)
    for copy in sent_weights:
        copy.wait_send()
    pltpu.make_async_copy(fin, out_ref.at[core], out_local).wait()
    last = pltpu.make_async_remote_copy(
        src_ref=fin, dst_ref=out_ref.at[other], send_sem=out_send, recv_sem=out_recv,
        device_id={"section": other}, device_id_type=MESH,
    )
    last.wait_send()
    last.wait_recv()


def shards(n, inputs, segments, gains, w_query, w_keyval, w_output):
    micro_count, tok, cols = inputs.shape
    width = gains.shape[-1]
    kvw = w_keyval.shape[-1]
    inner = inner_of(n)
    outer = n // inner
    half = HD // 2
    freqs = np.float32(rope_theta) ** (-(2.0 * np.arange(half, dtype=np.float32)) / np.float32(HD))
    freqs = np.broadcast_to(np.concatenate([freqs, freqs])[None].astype(np.float32), (8, HD))
    dma = pltpu.SemaphoreType.DMA
    vmem = pl.BlockSpec(memory_space=pltpu.VMEM)
    hbm = pl.BlockSpec(memory_space=pl.ANY)
    out = pl.pallas_call(
        functools.partial(kernel, n),
        out_shape=jax.ShapeDtypeStruct((micro_count, tok, cols), BF16),
        in_specs=[hbm, vmem, vmem, hbm, hbm, hbm, hbm],
        out_specs=hbm,
        scratch_shapes=[
            pltpu.VMEM((2, tok, width), BF16),
            pltpu.VMEM((2, width, HD), BF16),
            pltpu.VMEM((2, width, kvw), BF16),
            pltpu.VMEM((2,) + w_output.shape[2:], BF16),
            pltpu.VMEM((2, 1, width), BF16),
            pltpu.VMEM((2, n, 8, tok), F32),
            pltpu.VMEM((2, GROUP, tok, kvw), BF16),
            pltpu.VMEM((2, tok, n * HD), BF16),
            pltpu.VMEM((tok, cols), BF16),
            pltpu.VMEM((tok, HD + kvw), F32),
            pltpu.VMEM((tok, HD), F32),
            pltpu.VMEM((tok, HD), F32),
            pltpu.VMEM((tok, HD), F32),
            pltpu.VMEM((tok, tok), F32),
            dma,
            dma((2, 4)),
            dma((4,)),
            dma((2, n)),
            dma((2, 2, outer)),
            dma((2, max(inner, 2), outer)),
            dma((2, n)),
            dma((2, n)),
            dma((2, GROUP)),
            dma((2, GROUP)),
            dma((2, n)),
            dma((2, n)),
            dma,
            dma,
            dma,
        ],
        compiler_params=pltpu.CompilerParams(
            collective_id=0, has_side_effects=True, vmem_limit_bytes=60 * 1024 * 1024
        ),
    )(
        inputs, segments, jnp.asarray(freqs), gains[0], w_query[0, 0], w_keyval[0, 0], w_output[0, 0]
    )
    return out[None]


def solution(mesh):
    return jax.shard_map(
        functools.partial(shards, mesh.shape["mesh"]),
        mesh=mesh,
        in_specs=(
            P("groups", None, "mesh"),
            P("groups", None),
            P("section", None, None),
            P("section", None, None, "mesh"),
            P("section", None, None, "mesh"),
            P("section", None, None, "mesh"),
        ),
        out_specs=P("section", "groups", None, "mesh"),
        check_vma=False,
    )
```

time: 304 us -> 96.8 us (0.32)
  waiting for transfers between devices: 166 us -> 0 us
  Pallas kernels: 0 us -> 91.4 us
  blocking collectives: 79.6 us -> 0 us
  matrix products: 17.5 us -> 0 us
  other arithmetic: 14.2 us -> 0 us
  between operations: 13.5 us -> 0.01 us
  starting transfers between devices: 12.1 us -> 0 us
  local copies, waits for them, and re-layouts: 1.03 us -> 5.16 us
    all_gather x3 -> x0, waiting for transfers between devices: 142 us -> none  [apply_layer(): gathered = lax.all_gather(activations, 'mesh', axis=1, tiled=True)]
    pallas_call x0 -> x1, Pallas kernels: none -> 91.4 us  [shards(): pl.pallas_call(functools.partial(kernel, n), out_shape=jax.ShapeDtypeStru...]
    all_gather x3 -> x0, blocking collectives: 79.6 us -> none  [apply_layer(): lax.all_gather(attended, 'mesh', axis=1, tiled=True)]
    ppermute x11 -> x0, waiting for transfers between devices: 24.1 us -> none  [the longest x9 21.9 us: partner_2(): lax.ppermute(x, axis, [(i, i ^ 1 << distance) for i in range(lax.axis_siz...]
    dot_general x15 -> x0, matrix products: 17.5 us -> none  [the longest x3 9.91 us: apply_layer(): jnp.dot(normed, query_weight, preferred_element_type=jnp.float32)]
    ppermute x11 -> x0, starting transfers between devices: 12 us -> none  [the longest x9 9.36 us: partner_2(): lax.ppermute(x, axis, [(i, i ^ 1 << distance) for i in range(lax.axis_siz...]
    reduce_sum x6 -> x0, other arithmetic: 6.81 us -> none  [the longest x3 6.68 us: apply_layer(): jnp.mean(whole_floats * whole_floats, axis=1, keepdims=True) + norm_epsilon]
    unnamed x18 -> x4, local copies, waits for them, and re-layouts: 0.04 us -> 4.57 us
  transfers between devices with their start and end apart: 14 -> 0, of which waited for: 11 -> 0; matrix products, arithmetic and copies ran while one was open for 5% -> 0% of each run, Pallas kernels for 0% -> 0%
where the time goes in v1:
time: 96.8 us; the launch traced here: 96.6 us
  Pallas kernels  91.4 us (94%)
  local copies, waits for them, and re-layouts  5.16 us (5%)
    pallas_call x1, Pallas kernels, shards(): pl.pallas_call(functools.partial(kernel, n), out_shape=jax.ShapeDtypeStru...  91.4 us
    unnamed x4, local copies, waits for them, and re-layouts  4.57 us

profile of v1, /device:TPU:0, one launch (start us, length us, event | category | flops | bytes accessed | tf_op | source)
XLA Modules:
  0.0 96.6 jit_solution(5778674012289925941)
XLA Ops:
  0.0 0.0 copy-start
  0.0 2.7 %copy.8 = bf16[1,1,8192,32]{3,2,1,0:T(8,128)(2,1)} copy(bf16[1,1,8192,32]{2,3,1,0:T(8,128)(2,1)} %param.11) | data formatting | bytes 1048576 | tf_op args[4]
  2.7 0.0 copy-done
  2.7 0.6 jit_solution_.3.freq_ref
  3.3 91.4 %shard_map.73 = bf16[2,128,1024]{2,1,0:T(8,128)(2,1)} custom-call(bf16[2,128,1024]{2,1,0:T(8,128)(2,1)} %x_hbm.1, s32[2,128]{1,0:T(2,128)} %seg_ref.1, f32[8,128]{1,0:T(8,128)} %jit_solution_.3.freq_ref, bf16[1,8192]{1,0:T(2,128)(2,1)} %bitcast.9, bf16[8192,128]{1,0:T(8,128)(2,1)} %bitcast.6, bf16[8192,32]{1,0:T(8,128)(2,1)} %bitcast.5, ...), custom_call_target="tpu_custom_call" | custom-call | tf_op jit(solution)/shard_map/pallas_call | solution.py:349
  94.7 1.9 %copy.10 = bf16[1,2,128,1024]{3,2,1,0:T(8,128)(2,1)} copy(bf16[1,2,128,1024]{3,2,1,0:T(8,128)(2,1)} %bitcast.8) | data formatting | bytes 1048576
Async XLA Ops:
  0.0 2.7 %copy-start = (f32[128]{0:T(128)S(1)}, f32[128]{0:T(128)}, u32[]{:S(2)}) copy-start(f32[128]{0:T(128)} %constant.2.clone) | copy-start | bytes 1540

commit v2 on v1

--- a/solution.py
+++ b/solution.py
@@ -3,7 +3,6 @@
 
 import jax
 import jax.numpy as jnp
-import numpy as np
 from jax import lax
 from jax.experimental import pallas as pl
 from jax.experimental.pallas import tpu as pltpu
@@ -11,6 +10,7 @@
 
 HD = 128
 GROUP = 8
+CHUNKS = 2
 norm_epsilon = 1e-05
 rope_theta = 500000.0
 MESH = pl.DeviceIdType.MESH
@@ -29,7 +29,6 @@
     n,
     x_hbm,
     seg_ref,
-    freq_ref,
     g_hbm,
     wq_hbm,
     wkv_hbm,
@@ -45,6 +44,7 @@
     att,
     fin,
     acc,
+    acc_kv,
     scale_ref,
     cos_ref,
     sin_ref,
@@ -73,7 +73,7 @@
     row, lane = me // inner, me % inner
     tok, cols = x_hbm.shape[1:]
     width = n * cols
-    kvw = wkv_hbm.shape[1]
+    part = tok // CHUNKS
     first = me // GROUP * GROUP
 
     def block(layer, src):
@@ -112,20 +112,23 @@
     load_x.wait()
     pl.semaphore_wait(barrier, n)
 
-    def z_copy(layer, src, sign):
+    def chunk(layer, c, src):
+        return xbuf.at[layer, pl.ds(c * part, part), pl.ds(pl.multiple_of(src * cols, cols), cols)]
+
+    def z_copy(layer, c, src, sign):
         return send_to(
-            block(layer, src), block(layer, src), z_send.at[layer, (sign + 1) // 2, src // inner],
-            x_recv.at[layer, src], me + sign * inner,
-        )
-
-    def y_copy(layer, src, k):
+            chunk(layer, c, src), chunk(layer, c, src), z_send.at[layer, c, (sign + 1) // 2, src // inner],
+            x_recv.at[layer, c, src], me + sign * inner,
+        )
+
+    def y_copy(layer, c, src, k):
         return send_to(
-            block(layer, src), block(layer, src), y_send.at[layer, k, src // inner],
-            x_recv.at[layer, src], row * inner + (lane + k) % inner,
-        )
-
-    def arrived(layer, src):
-        y_copy(layer, src, 0).wait_recv()
+            chunk(layer, c, src), chunk(layer, c, src), y_send.at[layer, c, k, src // inner],
+            x_recv.at[layer, c, src], row * inner + (lane + k) % inner,
+        )
+
+    def arrived(layer, c, src):
+        y_copy(layer, c, src, 0).wait_recv()
 
     def over_y(body):
         if inner == 2:
@@ -136,12 +139,12 @@
                 return carry
             lax.fori_loop(1, inner, step, 0)
 
-    def forward(layer, src, signs):
+    def forward(layer, c, src, signs):
         for sign in signs:
             @pl.when((row + sign >= 0) & (row + sign < outer))
             def _():
-                z_copy(layer, src, sign).start()
-        over_y(lambda k: y_copy(layer, src, k).start())
+                z_copy(layer, c, src, sign).start()
+        over_y(lambda k: y_copy(layer, c, src, k).start())
 
     def over_peers(total, base, mine, body):
         def step(k, carry):
@@ -160,7 +163,8 @@
         total = jnp.sum(floats * floats, axis=1, keepdims=True)
         ssq[layer, me] = jnp.transpose(jnp.broadcast_to(total, (tok, tok)))[:8]
         over_peers(n, 0, me, lambda peer: ssq_copy(layer, peer).start())
-        forward(layer, me, (1, -1))
+        for c in range(CHUNKS):
+            forward(layer, c, me, (1, -1))
 
     send_own(0, block(0, me)[...])
     for copy in sent_weights:
@@ -172,10 +176,11 @@
     allowed = jnp.where((seg == jnp.transpose(seg)) & (u_index <= t_index), 1.0, 0.0)
     mask_ref[...] = allowed
     positions = jnp.sum(allowed, axis=1, keepdims=True) - 1.0
-    angles = positions * freq_ref[0:1, :]
+    head_lane = lax.broadcasted_iota(jnp.int32, (tok, HD), 1)
+    freqs = jnp.exp((head_lane % (HD // 2)).astype(F32) * (-2.0 * math.log(rope_theta) / HD))
+    angles = positions * freqs
     cos_ref[...] = jnp.cos(angles)
     sine = jnp.sin(angles)
-    head_lane = lax.broadcasted_iota(jnp.int32, (tok, HD), 1)
     sin_ref[...] = jnp.where(head_lane < HD // 2, -sine, sine)
 
     def rope(values):
@@ -189,8 +194,10 @@
         span = pl.ds(pl.multiple_of(src * cols, cols), cols)
         scale = jnp.concatenate([scale_ref[...]] * (cols // HD), axis=1)
         normed = (xbuf[layer, :, span].astype(F32) * scale * gbuf[layer, :, span].astype(F32)).astype(BF16)
-        both = jnp.concatenate([wq[layer, span, :], wkv[layer, span, :]], axis=1)
-        acc[...] += jnp.dot(normed, both, preferred_element_type=F32)
+        acc[...] += jnp.dot(normed, wq[layer, span, :], preferred_element_type=F32)
+        acc_kv[...] += lax.dot_general(
+            wkv[layer, :, span], normed, (((1,), (1,)), ((), ())), preferred_element_type=F32
+        )
 
     for layer in range(2):
         over_peers(n, 0, me, lambda peer: ssq_wait(layer, peer))
@@ -201,6 +208,7 @@
         for k in range(3):
             weight_wait(layer, k)
         acc[...] = jnp.zeros_like(acc)
+        acc_kv[...] = jnp.zeros_like(acc_kv)
         consume(layer, me)
 
         def side_blocks(distance):
@@ -211,20 +219,27 @@
                 def _():
                     def take(k):
                         src = src_row * inner + (lane + k) % inner
-                        arrived(layer, src)
+                        for c in range(CHUNKS):
+                            arrived(layer, c, src)
                         consume(layer, src)
                     over_y(take)
 
         def wave(distance, carry):
+            for c in range(CHUNKS):
+                for sign in (1, -1):
+                    src_row = row - sign * distance
+
+                    @pl.when((src_row >= 0) & (src_row < outer))
+                    def _():
+                        src = src_row * inner + lane
+                        arrived(layer, c, src)
+                        forward(layer, c, src, (sign,))
             for sign in (1, -1):
                 src_row = row - sign * distance
 
                 @pl.when((src_row >= 0) & (src_row < outer))
                 def _():
-                    src = src_row * inner + lane
-                    arrived(layer, src)
-                    forward(layer, src, (sign,))
-                    consume(layer, src)
+                    consume(layer, src_row * inner + lane)
 
             @pl.when(distance > 1)
             def _():
@@ -233,7 +248,8 @@
 
         def take_own_row(k):
             src = row * inner + (lane + k) % inner
-            arrived(layer, src)
+            for c in range(CHUNKS):
+                arrived(layer, c, src)
             consume(layer, src)
 
         lax.fori_loop(1, 2, wave, 0)
@@ -241,7 +257,7 @@
         lax.fori_loop(2, outer, wave, 0)
         side_blocks(outer - 1)
 
-        kvbuf[layer, me - first] = acc[:, HD:].astype(BF16)
+        kvbuf[layer, me - first] = acc_kv[...].astype(BF16)
 
         def kv_copy(peer):
             return send_to(
@@ -256,17 +272,19 @@
             ).wait_recv()
 
         over_peers(GROUP, first, me, lambda peer: kv_copy(peer).start())
-        query = rope(acc[:, :HD])
+        query = rope(acc[...])
         over_peers(GROUP, first, me, kv_wait)
-        keyval = jnp.concatenate([kvbuf[layer, j] for j in range(GROUP)], axis=1)
-        keys = rope(keyval[:, :HD].astype(F32))
+        keyval = jnp.concatenate([kvbuf[layer, j] for j in range(GROUP)], axis=0)
+        keys = rope(jnp.transpose(keyval[:HD].astype(F32)))
         scores = lax.dot_general(
             query, keys, (((1,), (1,)), ((), ())), preferred_element_type=F32
         ) * HD ** (-0.5)
         masked = jnp.where(mask_ref[...] > 0.0, scores, -1e30)
         raised = jnp.exp(masked - jnp.max(masked, axis=1, keepdims=True))
         probs = (raised / jnp.sum(raised, axis=1, keepdims=True)).astype(BF16)
-        attended = jnp.dot(probs, keyval[:, HD:], preferred_element_type=F32).astype(BF16)
+        attended = lax.dot_general(
+            probs, keyval[HD:], (((1,), (1,)), ((), ())), preferred_element_type=F32
+        ).astype(BF16)
 
         def att_block(src):
             return att.at[layer, :, pl.ds(pl.multiple_of(src * HD, HD), HD)]
@@ -308,21 +326,22 @@
     for layer in range(2):
         over_peers(n, 0, me, lambda peer: ssq_copy(layer, peer).wait_send())
 
-        def drain(src_row, carry):
-            src = src_row * inner + lane
-
-            @pl.when((src_row <= row) & (row + 1 < outer))
-            def _():
-                z_copy(layer, src, 1).wait_send()
-
-            @pl.when((src_row >= row) & (row >= 1))
-            def _():
-                z_copy(layer, src, -1).wait_send()
-
-            over_y(lambda k: y_copy(layer, src, k).wait_send())
-            return carry
-
-        lax.fori_loop(0, outer, drain, 0)
+        for c in range(CHUNKS):
+            def drain(src_row, carry):
+                src = src_row * inner + lane
+
+                @pl.when((src_row <= row) & (row + 1 < outer))
+                def _():
+                    z_copy(layer, c, src, 1).wait_send()
+
+                @pl.when((src_row >= row) & (row >= 1))
+                def _():
+                    z_copy(layer, c, src, -1).wait_send()
+
+                over_y(lambda k: y_copy(layer, c, src, k).wait_send())
+                return carry
+
+            lax.fori_loop(0, outer, drain, 0)
     for copy in sent_weights:
         copy.wait_send()
     pltpu.make_async_copy(fin, out_ref.at[core], out_local).wait()
@@ -340,28 +359,26 @@
     kvw = w_keyval.shape[-1]
     inner = inner_of(n)
     outer = n // inner
-    half = HD // 2
-    freqs = np.float32(rope_theta) ** (-(2.0 * np.arange(half, dtype=np.float32)) / np.float32(HD))
-    freqs = np.broadcast_to(np.concatenate([freqs, freqs])[None].astype(np.float32), (8, HD))
     dma = pltpu.SemaphoreType.DMA
     vmem = pl.BlockSpec(memory_space=pltpu.VMEM)
     hbm = pl.BlockSpec(memory_space=pl.ANY)
     out = pl.pallas_call(
         functools.partial(kernel, n),
         out_shape=jax.ShapeDtypeStruct((micro_count, tok, cols), BF16),
-        in_specs=[hbm, vmem, vmem, hbm, hbm, hbm, hbm],
+        in_specs=[hbm, vmem, hbm, hbm, hbm, hbm],
         out_specs=hbm,
         scratch_shapes=[
             pltpu.VMEM((2, tok, width), BF16),
             pltpu.VMEM((2, width, HD), BF16),
-            pltpu.VMEM((2, width, kvw), BF16),
+            pltpu.VMEM((2, kvw, width), BF16),
             pltpu.VMEM((2,) + w_output.shape[2:], BF16),
             pltpu.VMEM((2, 1, width), BF16),
             pltpu.VMEM((2, n, 8, tok), F32),
-            pltpu.VMEM((2, GROUP, tok, kvw), BF16),
+            pltpu.VMEM((2, GROUP, kvw, tok), BF16),
             pltpu.VMEM((2, tok, n * HD), BF16),
             pltpu.VMEM((tok, cols), BF16),
-            pltpu.VMEM((tok, HD + kvw), F32),
+            pltpu.VMEM((tok, HD), F32),
+            pltpu.VMEM((kvw, tok), F32),
             pltpu.VMEM((tok, HD), F32),
             pltpu.VMEM((tok, HD), F32),
             pltpu.VMEM((tok, HD), F32),
@@ -369,9 +386,9 @@
             dma,
             dma((2, 4)),
             dma((4,)),
-            dma((2, n)),
-            dma((2, 2, outer)),
-            dma((2, max(inner, 2), outer)),
+            dma((2, CHUNKS, n)),
+            dma((2, CHUNKS, 2, outer)),
+            dma((2, CHUNKS, max(inner, 2), outer)),
             dma((2, n)),
             dma((2, n)),
             dma((2, GROUP)),
@@ -386,7 +403,7 @@
             collective_id=0, has_side_effects=True, vmem_limit_bytes=60 * 1024 * 1024
         ),
     )(
-        inputs, segments, jnp.asarray(freqs), gains[0], w_query[0, 0], w_keyval[0, 0], w_output[0, 0]
+        inputs, segments, gains[0], w_query[0, 0], jnp.swapaxes(w_keyval[0, 0], 0, 1), w_output[0, 0]
     )
     return out[None]
 

time: 96.8 us -> 81.6 us (0.84)
  Pallas kernels: 91.4 us -> 79.6 us
  local copies, waits for them, and re-layouts: 5.16 us -> 1.87 us
    pallas_call x1, Pallas kernels: 91.4 us -> 79.6 us  [shards(): pl.pallas_call(functools.partial(kernel, n), out_shape=jax.ShapeDtypeStru...]
    unnamed x4 -> x1, local copies, waits for them, and re-layouts: 4.57 us -> 1.87 us
where the time goes in v2:
time: 81.6 us; the launch traced here: 81.5 us
  Pallas kernels  79.6 us (98%)
  local copies, waits for them, and re-layouts  1.87 us (2%)
    pallas_call x1, Pallas kernels, shards(): pl.pallas_call(functools.partial(kernel, n), out_shape=jax.ShapeDtypeStru...  79.6 us
    unnamed x1, local copies, waits for them, and re-layouts  1.87 us

profile of v2, /device:TPU:0, one launch (start us, length us, event | category | flops | bytes accessed | tf_op | source)
XLA Modules:
  0.0 81.5 jit_solution(17579673251263872488)
XLA Ops:
  0.0 79.6 %shard_map.64 = bf16[2,128,1024]{2,1,0:T(8,128)(2,1)} custom-call(bf16[2,128,1024]{2,1,0:T(8,128)(2,1)} %x_hbm.1, s32[2,128]{1,0:T(2,128)} %seg_ref.1, bf16[1,8192]{1,0:T(2,128)(2,1)} %bitcast.11, bf16[8192,128]{1,0:T(8,128)(2,1)} %bitcast.7, bf16[32,8192]{1,0:T(8,128)(2,1)} %bitcast.10, bf16[1024,1024]{1,0:T(8,128)(2,1)} %bitcast.8), custom_call_target="tpu_custom_call" | custom-call | tf_op jit(solution)/shard_map/pallas_call | solution.py:365
  79.6 1.9 %copy.8 = bf16[1,2,128,1024]{3,2,1,0:T(8,128)(2,1)} copy(bf16[1,2,128,1024]{3,2,1,0:T(8,128)(2,1)} %bitcast.9) | data formatting | bytes 1048576
